TPU v7x, 32 devices: a whole 2x2x4 slice. The times are simulated.
32 devices in a mesh: rep: 4 (over z), row: 4 (over x, core), col: 2 (over y).
Axes of the slice: x: 2, y: 2, z: 4, core: 2. Of those that a mesh axis runs over, the one named last changes fastest.
Arguments:
- grad_parts: bfloat16 [4, 16384, 6144], P('rep', ('row', 'col')), may hold values from -0.03125 to 0.03125, as said below
- statistic: float32 [6144, 6144], P('row', 'col'), may hold values from -150 to 150, as said below
Outputs:
- gram_matrix: float32 [6144, 6144], P('row', 'col')
- statistic_next: float32 [6144, 6144], P('row', 'col')
Inputs may be any that keep to these rules, and one draw needn't show every extreme that they name: Every entry of grad_parts has a magnitude between 2^-10 and 2^-5. statistic is symmetric and positive definite.
All inputs are finite; a program needn't handle non-finite values.
Results may differ from a plain program's by a relative error of at most 0.008.
Values may be sent and summed in bfloat16 or wider, within the bound.
A program may use at most 192 MiB of HBM per device.

v0:
```python
import jax
import jax.numpy as jnp
from jax import lax
from jax.sharding import PartitionSpec as P


def shards(grad_parts, statistic):
    own_part = grad_parts[0].astype(jnp.float32)
    summed = lax.psum_scatter(own_part.astype(jnp.bfloat16), "rep", scatter_dimension=0, tiled=True)
    rows_panel = lax.all_to_all(summed, "row", split_axis=1, concat_axis=0, tiled=True)
    cols_panel = lax.all_to_all(summed, "col", split_axis=1, concat_axis=0, tiled=True)
    row_count = lax.axis_size("row")
    col_count = lax.axis_size("col")
    quarter = summed.shape[0]
    left_whole = lax.all_gather(rows_panel, "col", axis=0, tiled=True)
    left_order = (
        left_whole.reshape(col_count, row_count, quarter, -1)
        .transpose(1, 0, 2, 3)
        .reshape(row_count * col_count * quarter, -1)
    )
    partial_tile = lax.dot_general(
        left_order,
        lax.all_gather(cols_panel, "row", axis=0, tiled=True),
        (((0,), (0,)), ((), ())),
        preferred_element_type=jnp.float32,
    )
    gram_tile = lax.psum(partial_tile, "rep")
    return (gram_tile, 0.95 * statistic + 0.05 * gram_tile)


def solution(mesh):
    return jax.shard_map(
        shards,
        mesh=mesh,
        in_specs=(P("rep", ("row", "col"), None), P("row", "col")),
        out_specs=(P("row", "col"), P("row", "col")),
        check_vma=False,
    )
```

profile of v0, /device:TPU:0, one launch (start us, length us, event | category | flops | bytes accessed | tf_op | source)
XLA Modules:
  0.0 1626.5 jit_solution(12246390620208611394)
XLA Ops:
  7.2 0.0 reduce-scatter.2.cloned.1.call-start
  7.2 30.3 %copy.5 = bf16[1,2048,6144]{1,2,0:T(8,128)(2,1)} copy(bf16[1,2048,6144]{2,1,0:T(8,128)(2,1)} %param.2) | data formatting | bytes 50331648 | tf_op args[0]
  37.5 0.0 reduce-scatter.2.cloned.1.call-update
  37.6 0.0 all-gather.3.cloned.1.call-start
  37.6 417.0 %reduce-scatter.2.cloned.1.call-done = bf16[512,6144]{0,1:T(8,128)(2,1)} async-done(((bf16[2048,6144]{0,1:T(8,128)(2,1)}), bf16[512,6144]{0,1:T(8,128)(2,1)}) %reduce-scatter.2.cloned.1.call-update) | async-done | bytes 6291472 | tf_op jit(solution)/shard_map/reduce_scatter | solution.py:9
  454.7 77.3 %all_to_all.38 = bf16[512,4,1536]{0,2,1:T(8,128)(2,1)} all-to-all(bf16[512,4,1536]{0,2,1:T(8,128)(2,1)} %bitcast.15), channel_id=1, replica_groups=mesh['rep'=4,'row'=4,'col'=2] {'row'}, dimensions={1} | all-to-all | bytes 12582912 | tf_op jit(solution)/shard_map/all_to_all | solution.py:10
  532.0 8.6 copy.6
  540.6 0.0 all-gather.3.cloned.1.call-update
  540.6 0.0 all-gather.5.cloned.1.call-start
  540.7 140.8 %all_to_all.39 = bf16[512,2,3072]{0,2,1:T(8,128)(2,1)} all-to-all(bf16[512,2,3072]{0,2,1:T(8,128)(2,1)} %bitcast.16), channel_id=1, replica_groups=mesh['rep'=4,'row'=4,'col'=2] {'col'}, dimensions={1} | all-to-all | bytes 12582912 | tf_op jit(solution)/shard_map/all_to_all | solution.py:11
  681.4 8.6 copy.8
  690.1 0.0 all-gather.5.cloned.1.call-update
  690.1 0.0 all-reduce.2.cloned.1.call-start
  690.2 64.5 %all-gather.3.cloned.1.call-done = bf16[4096,1536]{1,0:T(8,128)(2,1)} async-done(((bf16[2048,1536]{1,0:T(8,128)(2,1)}), bf16[4096,1536]{1,0:T(8,128)(2,1)}) %all-gather.3.cloned.1.call-update) | async-done | bytes 12582928 | tf_op jit(solution)/shard_map/all_gather | solution.py:15
  754.7 11.1 copy.7
  765.8 145.7 %all-gather.5.cloned.1.call-done = bf16[4096,3072]{1,0:T(8,128)(2,1)} async-done(((bf16[1024,3072]{1,0:T(8,128)(2,1)}), bf16[4096,3072]{1,0:T(8,128)(2,1)}) %all-gather.5.cloned.1.call-update) | async-done | bytes 25165840 | tf_op jit(solution)/shard_map/all_gather | solution.py:23
  911.5 48.0 %fusion = f32[1536,3072]{1,0:T(8,128)} fusion(bf16[4096,1536]{1,0:T(8,128)(2,1)} %bitcast.21, bf16[4096,3072]{1,0:T(8,128)(2,1)} %all-gather.5.cloned.1.call-done), kind=kOutput, calls=%fused_computation.1 | convolution fusion | flops 38654705664 | bytes 56623104 | tf_op jit(solution)/shard_map/dot_general | solution.py:21
  959.5 0.0 all-reduce.2.cloned.1.call-update
  959.6 629.5 %all-reduce.2.cloned.1.call-done = f32[1536,3072]{1,0:T(8,128)} async-done(((f32[1536,3072]{1,0:T(8,128)}), f32[1536,3072]{1,0:T(8,128)}) %all-reduce.2.cloned.1.call-update) | async-done | bytes 18874384 | tf_op jit(solution)/shard_map/psum | solution.py:27
  1589.1 0.0 copy-start
  1589.1 20.7 %multiply_add_fusion = f32[1536,3072]{1,0:T(8,128)} fusion(f32[1536,3072]{1,0:T(8,128)} %all-reduce.2.cloned.1.call-done, f32[1536,3072]{1,0:T(8,128)} %param.3), kind=kLoop, calls=%fused_computation | loop fusion | flops 14155776 | bytes 56623104 | tf_op jit(solution)/shard_map/add | solution.py:28
  1609.8 3.3 copy-done
  1613.1 6.8 copy.10
Async XLA Ops:
  7.2 447.5 %reduce-scatter.2.cloned.1.call-start = ((), (), s32[]{:S(2)}) async-start(), calls=%async_computation.3 | async-start | bytes 31457280 | tf_op jit(solution)/shard_map/reduce_scatter | solution.py:9
  37.6 717.1 %all-gather.3.cloned.1.call-start = ((), (), s32[]{:S(2)}) async-start(), calls=%async_computation.4 | async-start | bytes 18874368 | tf_op jit(solution)/shard_map/all_gather | solution.py:15
  540.6 370.9 %all-gather.5.cloned.1.call-start = ((), (), s32[]{:S(2)}) async-start(), calls=%async_computation.5 | async-start | bytes 31457280 | tf_op jit(solution)/shard_map/all_gather | solution.py:23
  690.1 899.0 %all-reduce.2.cloned.1.call-start = ((), (), s32[]{:S(2)}) async-start(), calls=%async_computation.6 | async-start | bytes 37748736 | tf_op jit(solution)/shard_map/psum | solution.py:27
  1589.1 24.0 %copy-start = (f32[1536,3072]{1,0:T(8,128)S(1)}, f32[1536,3072]{1,0:T(8,128)}, u32[]{:S(2)}) copy-start(f32[1536,3072]{1,0:T(8,128)} %all-reduce.2.cloned.1.call-done) | copy-start | bytes 56623108
Sparse Core Ops, SparseCore 0:
  37.7 416.9 reduce-scatter.1
  540.7 213.8 all-gather.2
  756.2 155.2 all-gather.4
  959.7 629.3 all-reduce.1
where the time goes:
time: 1630 us
  waiting for transfers between devices  1260 us (77%)
  blocking collectives  218 us (13%)
  local copies, waits for them, and re-layouts  68.9 us (4%)
  matrix products  48 us (3%)
  other arithmetic  20.7 us (1%)
    psum x1, waiting for transfers between devices, shards(): gram_tile = lax.psum(partial_tile, 'rep')  630 us
    reduce_scatter x1, waiting for transfers between devices, shards(): lax.psum_scatter(own_part.astype(jnp.bfloat16), 'rep', scatter_dimension=...  417 us
    all_gather x1, waiting for transfers between devices, shards(): lax.all_gather(cols_panel, 'row', axis=0, tiled=True)  146 us
    all_to_all x1, blocking collectives, shards(): lax.all_to_all(summed, 'col', split_axis=1, concat_axis=0, tiled=True)  141 us
    all_to_all x1, blocking collectives, shards(): lax.all_to_all(summed, 'row', split_axis=1, concat_axis=0, tiled=True)  77.3 us
    all_gather x1, waiting for transfers between devices, shards(): left_whole = lax.all_gather(rows_panel, 'col', axis=0, tiled=True)  64.5 us
    dot_general x1, matrix products, shards(): lax.dot_general(left_order, lax.all_gather(cols_panel, 'row', axis=0, til...  48 us
    unnamed x4, local copies, waits for them, and re-layouts  40.5 us
  transfers between devices with their start and end apart: 4, of which 4 were waited for; matrix products, arithmetic and copies ran while one was open for 1% of the time, Pallas kernels for 0%

commit v1 on v0

--- a/solution.py
+++ b/solution.py
@@ -2,6 +2,14 @@
 import jax.numpy as jnp
 from jax import lax
 from jax.sharding import PartitionSpec as P
+
+
+def doubling_sum(x, axis):
+    peers, total = (lax.axis_size(axis), x)
+    for far in [1 << k for k in range(peers.bit_length() - 1)]:
+        route = [(i, i ^ far) for i in range(peers)]
+        total = total + lax.ppermute(total, axis, route)
+    return total
 
 
 def shards(grad_parts, statistic):
@@ -24,7 +32,7 @@
         (((0,), (0,)), ((), ())),
         preferred_element_type=jnp.float32,
     )
-    gram_tile = lax.psum(partial_tile, "rep")
+    gram_tile = doubling_sum(partial_tile, "rep")
     return (gram_tile, 0.95 * statistic + 0.05 * gram_tile)
 
 

time: 1630 us -> 2240 us (1.37)
  waiting for transfers between devices: 1260 us -> 1840 us
  other arithmetic: 20.7 us -> 45.8 us
    ppermute x0 -> x2, waiting for transfers between devices: none -> 1220 us  [doubling_sum(): total = total + lax.ppermute(total, axis, route)]
    psum x1 -> x0, waiting for transfers between devices: 630 us -> none  [shards(): gram_tile = lax.psum(partial_tile, 'rep')]
  transfers between devices with their start and end apart: 4 -> 5, of which waited for: 4 -> 5; matrix products, arithmetic and copies ran while one was open for 1% -> 1% of each run, Pallas kernels for 0% -> 0%
where the time goes in v1:
time: 2240 us
  waiting for transfers between devices  1840 us (82%)
  blocking collectives  218 us (10%)
  local copies, waits for them, and re-layouts  65.5 us (3%)
  matrix products  48 us (2%)
  other arithmetic  45.8 us (2%)
    ppermute x2, waiting for transfers between devices, doubling_sum(): total = total + lax.ppermute(total, axis, route)  1220 us
    reduce_scatter x1, waiting for transfers between devices, shards(): lax.psum_scatter(own_part.astype(jnp.bfloat16), 'rep', scatter_dimension=...  417 us
    all_gather x1, waiting for transfers between devices, shards(): lax.all_gather(cols_panel, 'row', axis=0, tiled=True)  146 us
    all_to_all x1, blocking collectives, shards(): lax.all_to_all(summed, 'col', split_axis=1, concat_axis=0, tiled=True)  141 us
    all_to_all x1, blocking collectives, shards(): lax.all_to_all(summed, 'row', split_axis=1, concat_axis=0, tiled=True)  77.3 us
    all_gather x1, waiting for transfers between devices, shards(): left_whole = lax.all_gather(rows_panel, 'col', axis=0, tiled=True)  64.6 us
    dot_general x1, matrix products, shards(): lax.dot_general(left_order, lax.all_gather(cols_panel, 'row', axis=0, til...  48 us
  transfers between devices with their start and end apart: 5, of which 5 were waited for; matrix products, arithmetic and copies ran while one was open for 1% of the time, Pallas kernels for 0%

profile of v1, /device:TPU:0, one launch (start us, length us, event | category | flops | bytes accessed | tf_op | source)
XLA Modules:
  0.0 2238.2 jit_solution(3496893413869900209)
XLA Ops:
  7.2 0.0 reduce-scatter.2.cloned.1.call-start
  7.2 30.2 %copy.5 = bf16[1,2048,6144]{1,2,0:T(8,128)(2,1)} copy(bf16[1,2048,6144]{2,1,0:T(8,128)(2,1)} %param.2) | data formatting | bytes 50331648 | tf_op args[0]
  37.4 0.0 reduce-scatter.2.cloned.1.call-update
  37.5 0.0 all-gather.3.cloned.1.call-start
  37.5 417.0 %reduce-scatter.2.cloned.1.call-done = bf16[512,6144]{0,1:T(8,128)(2,1)} async-done(((bf16[2048,6144]{0,1:T(8,128)(2,1)}), bf16[512,6144]{0,1:T(8,128)(2,1)}) %reduce-scatter.2.cloned.1.call-update) | async-done | bytes 6291472 | tf_op jit(solution)/shard_map/reduce_scatter | solution.py:17
  454.6 77.3 %all_to_all.38 = bf16[512,4,1536]{0,2,1:T(8,128)(2,1)} all-to-all(bf16[512,4,1536]{0,2,1:T(8,128)(2,1)} %bitcast.14), channel_id=1, replica_groups=mesh['rep'=4,'row'=4,'col'=2] {'row'}, dimensions={1} | all-to-all | bytes 12582912 | tf_op jit(solution)/shard_map/all_to_all | solution.py:18
  531.9 8.6 copy.6
  540.5 0.0 all-gather.3.cloned.1.call-update
  540.5 0.0 all-gather.5.cloned.1.call-start
  540.6 140.7 %all_to_all.39 = bf16[512,2,3072]{0,2,1:T(8,128)(2,1)} all-to-all(bf16[512,2,3072]{0,2,1:T(8,128)(2,1)} %bitcast.15), channel_id=1, replica_groups=mesh['rep'=4,'row'=4,'col'=2] {'col'}, dimensions={1} | all-to-all | bytes 12582912 | tf_op jit(solution)/shard_map/all_to_all | solution.py:19
  681.3 8.7 copy.8
  690.0 0.0 all-gather.5.cloned.1.call-update
  690.0 64.6 %all-gather.3.cloned.1.call-done = bf16[4096,1536]{1,0:T(8,128)(2,1)} async-done(((bf16[2048,1536]{1,0:T(8,128)(2,1)}), bf16[4096,1536]{1,0:T(8,128)(2,1)}) %all-gather.3.cloned.1.call-update) | async-done | bytes 12582928 | tf_op jit(solution)/shard_map/all_gather | solution.py:23
  754.5 11.1 copy.7
  765.7 145.7 %all-gather.5.cloned.1.call-done = bf16[4096,3072]{1,0:T(8,128)(2,1)} async-done(((bf16[1024,3072]{1,0:T(8,128)(2,1)}), bf16[4096,3072]{1,0:T(8,128)(2,1)}) %all-gather.5.cloned.1.call-update) | async-done | bytes 25165840 | tf_op jit(solution)/shard_map/all_gather | solution.py:31
  911.4 48.0 %fusion = f32[1536,3072]{1,0:T(8,128)} fusion(bf16[4096,1536]{1,0:T(8,128)(2,1)} %bitcast.21, bf16[4096,3072]{1,0:T(8,128)(2,1)} %all-gather.5.cloned.1.call-done), kind=kOutput, calls=%fused_computation.1 | convolution fusion | flops 38654705664 | bytes 56623104 | tf_op jit(solution)/shard_map/dot_general | solution.py:29
  959.4 1.5 collective-permute-start
  960.9 406.1 %collective-permute-done = f32[1536,3072]{1,0:T(8,128)} collective-permute-done((f32[1536,3072]{1,0:T(8,128)}, f32[1536,3072]{1,0:T(8,128)}, u32[]{:S(2)}, u32[]{:S(2)}) %collective-permute-start) | collective-permute-done | bytes 18874400 | tf_op jit(solution)/shard_map/ppermute | solution.py:11
  1367.1 12.6 add.11
  1379.7 0.0 copy-start
  1379.7 6.8 copy-done
  1386.5 2.4 collective-permute-start.1
  1388.9 809.5 %collective-permute-done.1 = f32[1536,3072]{1,0:T(8,128)} collective-permute-done((f32[1536,3072]{1,0:T(8,128)S(1)}, f32[1536,3072]{1,0:T(8,128)}, u32[]{:S(2)}, u32[]{:S(2)}) %collective-permute-start.1) | collective-permute-done | bytes 18874400 | tf_op jit(solution)/shard_map/ppermute | solution.py:11
  2198.4 33.2 %multiply_add_fusion = (f32[1536,3072]{1,0:T(8,128)}, f32[1536,3072]{1,0:T(8,128)}) fusion(f32[1536,3072]{1,0:T(8,128)} %param.3, f32[1536,3072]{1,0:T(8,128)} %copy-done, f32[1536,3072]{1,0:T(8,128)} %collective-permute-done.1), kind=kLoop, calls=%fused_computation | loop fusion | flops 18874368 | bytes 94371840 | tf_op jit(solution)/shard_map/add | solution.py:36
Async XLA Ops:
  7.2 447.4 %reduce-scatter.2.cloned.1.call-start = ((), (), s32[]{:S(2)}) async-start(), calls=%async_computation.3 | async-start | bytes 31457280 | tf_op jit(solution)/shard_map/reduce_scatter | solution.py:17
  37.5 717.1 %all-gather.3.cloned.1.call-start = ((), (), s32[]{:S(2)}) async-start(), calls=%async_computation.4 | async-start | bytes 18874368 | tf_op jit(solution)/shard_map/all_gather | solution.py:23
  540.5 370.9 %all-gather.5.cloned.1.call-start = ((), (), s32[]{:S(2)}) async-start(), calls=%async_computation.5 | async-start | bytes 31457280 | tf_op jit(solution)/shard_map/all_gather | solution.py:31
  959.4 407.6 %collective-permute-start = (f32[1536,3072]{1,0:T(8,128)}, f32[1536,3072]{1,0:T(8,128)}, u32[]{:S(2)}, u32[]{:S(2)}) collective-permute-start(f32[1536,3072]{1,0:T(8,128)} %fusion), channel_id=1, source_target_pairs={{0,8},{8,0},{16,24},{24,16},{1,9},{9,1},{17,25},{25,17},{2,10},{10... | collective-permute-start | bytes 56623112 | tf_op jit(solution)/shard_map/ppermute | solution.py:11
  1379.7 6.9 copy-start
  1386.5 811.9 %collective-permute-start.1 = (f32[1536,3072]{1,0:T(8,128)S(1)}, f32[1536,3072]{1,0:T(8,128)}, u32[]{:S(2)}, u32[]{:S(2)}) collective-permute-start(f32[1536,3072]{1,0:T(8,128)S(1)} %add.11), channel_id=1, source_target_pairs={{0,16},{8,24},{16,0},{24,8},{1,17},{9,25},{17,1},{25,9},{2,18},{10... | collective-permute-start | bytes 56623112 | tf_op jit(solution)/shard_map/ppermute | solution.py:11
Sparse Core Ops, SparseCore 0:
  37.6 416.9 reduce-scatter.1
  540.6 213.8 all-gather.2
  756.1 155.2 all-gather.4
